TPU v7x, 32 devices: a whole 2x2x4 slice. The times are simulated.
32 devices in a mesh: member: 2 (over x), dp: 16 (over z, y, core).
Axes of the slice: x: 2, y: 2, z: 4, core: 2. Of those that a mesh axis runs over, the one named last changes fastest.
Arguments:
- residual: bfloat16 [512, 3072], P(('member', 'dp')), parts along dimension 0, may hold values from -6 to 6
- upstream: bfloat16 [512, 3072], P(('member', 'dp')), parts along dimension 0, may hold values from -6 to 6
- gate_weight: bfloat16 [6144, 10240], P('member', 'dp'), parts along dimension 0, may hold values from -0.109375 to 0.109375
- up_weight: bfloat16 [6144, 10240], P('member', 'dp'), parts along dimension 0, may hold values from -0.109375 to 0.109375
- down_weight: bfloat16 [20480, 3072], P(('member', 'dp')), parts along dimension 0, may hold values from -0.0625 to 0.0625
- gain: float32 [6144], P('member'), parts along dimension 0, may hold values from 0.25 to 1.75
Outputs:
- grad_residual: bfloat16 [512, 3072], P(('member', 'dp')), parts along dimension 0
- grad_gate: bfloat16 [6144, 10240], P('member', 'dp'), parts along dimension 0
- grad_up: bfloat16 [6144, 10240], P('member', 'dp'), parts along dimension 0
- grad_down: bfloat16 [20480, 3072], P(('member', 'dp')), parts along dimension 0
- grad_gain: float32 [6144], P('member'), parts along dimension 0
There are 2 independent parts, one for each index of `member`. A program takes and returns all parts, laid end to end along the dimension named above; each array names one. Nothing has to cross between parts.
All inputs are finite; a program needn't handle non-finite values.
Results may differ from a plain program's by a relative error of at most 0.0068.
Values may be sent and summed in bfloat16 or wider, within the bound.
A program may use at most 128 MiB of HBM per device.

v0:
```python
import jax
import jax.numpy as jnp
from jax import lax
from jax.sharding import PartitionSpec as P

norm_floor = 0.5
gelu_coeff = 0.7978845608
cubic_term = 0.044715


def gelu_parts(gate_out):
    inner = jnp.tanh(gelu_coeff * (gate_out + cubic_term * gate_out * gate_out * gate_out))
    activated = 0.5 * gate_out * (1.0 + inner)
    gelu_slope = 0.5 * (1.0 + inner) + 0.5 * gate_out * (1.0 - inner * inner) * gelu_coeff * (
        1.0 + 3.0 * cubic_term * gate_out * gate_out
    )
    return (activated, gelu_slope)


def contract_last(left, right):
    return lax.dot_general(
        left, right, (((1,), (1,)), ((), ())), preferred_element_type=jnp.float32
    )


def contract_first(left, right):
    return lax.dot_general(
        left, right, (((0,), (0,)), ((), ())), preferred_element_type=jnp.float32
    )


def per_device(residual, upstream, gate_weight, up_weight, down_weight, gain):
    widened = residual.astype(jnp.float32)
    norm_scale = lax.rsqrt(jnp.mean(widened * widened, axis=1, keepdims=True) + norm_floor)
    unit_rows = widened * norm_scale
    normed = (unit_rows * gain).astype(jnp.bfloat16)
    normed_all = lax.all_gather(normed, "dp", axis=0, tiled=True)
    gate_out = jnp.dot(normed_all, gate_weight, preferred_element_type=jnp.float32)
    up_out = jnp.dot(normed_all, up_weight, preferred_element_type=jnp.float32)
    activated, gelu_slope = gelu_parts(gate_out)
    hidden = (activated * up_out).astype(jnp.bfloat16)
    upstream_all = lax.all_gather(upstream, "dp", axis=0, tiled=True)
    hidden_grad = contract_last(upstream_all, down_weight)
    grad_down = contract_first(hidden, upstream_all).astype(jnp.bfloat16)
    gate_grad = (hidden_grad * up_out * gelu_slope).astype(jnp.bfloat16)
    up_grad = (hidden_grad * activated).astype(jnp.bfloat16)
    grad_gate = contract_first(normed_all, gate_grad).astype(jnp.bfloat16)
    grad_up = contract_first(normed_all, up_grad).astype(jnp.bfloat16)
    partial_grad = contract_last(gate_grad, gate_weight) + contract_last(up_grad, up_weight)
    normed_grad = lax.psum_scatter(partial_grad, "dp", scatter_dimension=0, tiled=True)
    unit_grad = normed_grad * gain
    inner_mean = jnp.mean(unit_grad * unit_rows, axis=1, keepdims=True)
    grad_residual = (
        upstream.astype(jnp.float32) + norm_scale * (unit_grad - unit_rows * inner_mean)
    ).astype(jnp.bfloat16)
    grad_gain = lax.psum(jnp.sum(normed_grad * unit_rows, axis=0), "dp")
    return (grad_residual, grad_gate, grad_up, grad_down, grad_gain)


def solution(mesh):
    placed = (
        P(("member", "dp"), None),
        P(("member", "dp"), None),
        P("member", "dp"),
        P("member", "dp"),
        P(("member", "dp"), None),
        P("member"),
    )
    return jax.shard_map(
        per_device,
        mesh=mesh,
        in_specs=placed,
        out_specs=(
            P(("member", "dp"), None),
            P("member", "dp"),
            P("member", "dp"),
            P(("member", "dp"), None),
            P("member"),
        ),
        check_vma=False,
    )
```

profile of v0, /device:TPU:0, one launch (start us, length us, event | category | flops | bytes accessed | tf_op | source)
XLA Modules:
  0.0 235.7 jit_solution(8409215572186535631)
XLA Ops:
  7.2 0.0 all-gather.5.cloned.1.call-start
  7.2 1.0 fusion.18
  8.3 1.6 fusion.11
  9.9 0.0 all-gather.5.cloned.1.call-update
  9.9 0.0 all-gather.3.cloned.1.call-start
  10.0 0.7 all-gather.3.cloned.1.call-update
  10.7 0.0 reduce-scatter.2.cloned.1.call-start
  10.7 42.5 %all-gather.5.cloned.1.call-done = bf16[256,3072]{1,0:T(8,128)(2,1)} async-done(((bf16[16,3072]{1,0:T(8,128)(2,1)}), bf16[256,3072]{1,0:T(8,128)(2,1)}) %all-gather.5.cloned.1.call-update) | async-done | bytes 1572880 | tf_op jit(solution)/shard_map/all_gather | solution.py:37
  53.2 0.0 copy-start
  53.2 0.0 copy-start.2
  53.2 4.1 %fusion.24 = f32[256,640]{1,0:T(8,128)S(1)} fusion(bf16[256,3072]{1,0:T(8,128)(2,1)} %all-gather.5.cloned.1.call-done, bf16[3072,640]{1,0:T(8,128)(2,1)} %param.8), kind=kOutput, calls=%fused_computation.37 | convolution fusion | flops 1006632960 | bytes 6160384 | tf_op jit(solution)/shard_map/dot_general | solution.py:38
  57.3 0.0 copy-done
  57.3 0.1 copy-done.2
  57.4 1.5 fusion.23
  58.9 34.9 %all-gather.3.cloned.1.call-done = bf16[256,3072]{1,0:T(8,128)(2,1)} async-done(((bf16[16,3072]{1,0:T(8,128)(2,1)}), bf16[256,3072]{1,0:T(8,128)(2,1)}) %all-gather.3.cloned.1.call-update) | async-done | bytes 1572880 | tf_op jit(solution)/shard_map/all_gather | solution.py:42
  93.8 0.0 copy-start.1
  93.8 4.4 %multiply_convert_fusion.1 = (bf16[256,640]{1,0:T(8,128)(2,1)S(1)}, bf16[256,640]{1,0:T(8,128)(2,1)S(1)}) fusion(f32[256,640]{1,0:T(8,128)S(1)} %fusion.24, f32[256,640]{1,0:T(8,128)S(1)} %fusion.23, bf16[256,3072]{1,0:T(8,128)(2,1)} %all-gather.3.cloned.1.call-done, bf16[640,3072]{1,0:T(8,128)(2,1)} %param.10), kind=kOutput, calls=%fused_computation.14 | convolution fusion | flops 1010401280 | bytes 7471104 | tf_op jit(solution)/shard_map/dot_general | solution.py:21
  98.3 0.0 copy-start.3
  98.3 0.0 copy-done.1
  98.3 1.4 fusion.25
  99.7 0.7 copy-done.3
  100.4 3.1 %convolution_add_fusion = f32[256,3072]{1,0:T(8,128)} fusion(f32[256,3072]{1,0:T(8,128)S(1)} %fusion.25, bf16[256,640]{1,0:T(8,128)(2,1)S(1)} %get-tuple-element.7, bf16[3072,640]{1,0:T(8,128)(2,1)S(1)} %copy-done.3), kind=kOutput, calls=%fused_computation.3 | convolution fusion | flops 1007419392 | bytes 10551296 | tf_op jit(solution)/shard_map/dot_general | solution.py:21
  103.4 0.0 reduce-scatter.2.cloned.1.call-update
  103.5 3.4 %convolution_convert_fusion.1 = bf16[3072,640]{1,0:T(8,128)(2,1)} fusion(bf16[256,3072]{1,0:T(8,128)(2,1)S(1)} %copy-done, bf16[256,640]{1,0:T(8,128)(2,1)S(1)} %get-tuple-element.7), kind=kOutput, calls=%fused_computation.1 | convolution fusion | flops 1008599040 | bytes 5832704 | tf_op jit(solution)/shard_map/dot_general | solution.py:27
  106.8 0.0 copy-start.5
  106.8 3.4 %convolution_convert_fusion.2 = bf16[3072,640]{1,0:T(8,128)(2,1)} fusion(bf16[256,3072]{1,0:T(8,128)(2,1)S(1)} %copy-done, bf16[256,640]{1,0:T(8,128)(2,1)S(1)} %get-tuple-element.8), kind=kOutput, calls=%fused_computation.2 | convolution fusion | flops 1008599040 | bytes 5832704 | tf_op jit(solution)/shard_map/dot_general | solution.py:27
  110.2 0.0 copy-done.5
  110.2 0.0 copy-start.4
  110.2 0.0 copy-start.7
  110.2 0.0 copy-start.6
  110.2 3.3 %convolution_convert_fusion = bf16[640,3072]{1,0:T(8,128)(2,1)} fusion(bf16[256,3072]{1,0:T(8,128)(2,1)S(1)} %copy-done.5, f32[256,640]{1,0:T(8,128)S(1)} %fusion.23, f32[256,640]{1,0:T(8,128)S(1)} %fusion.24), kind=kOutput, calls=%fused_computation | convolution fusion | flops 1010237440 | bytes 6815744 | tf_op jit(solution)/shard_map/dot_general | solution.py:27
  113.5 55.1 %reduce-scatter.2.cloned.1.call-done = f32[16,3072]{1,0:T(8,128)} async-done(((f32[256,3072]{1,0:T(8,128)}), f32[16,3072]{1,0:T(8,128)}) %reduce-scatter.2.cloned.1.call-update) | async-done | bytes 196624 | tf_op jit(solution)/shard_map/reduce_scatter | solution.py:50
  168.6 0.0 copy-done.4
  168.6 0.0 copy-done.7
  168.6 1.2 fusion.17
  169.8 57.7 %psum.7 = f32[3072]{0:T(1024)} all-reduce(f32[3072]{0:T(1024)S(1)} %get-tuple-element.5), channel_id=1, replica_groups=mesh['member'=2,'dp'=16] {'dp'}, use_global_device_ids=true, to_apply=%region_4.0 | all-reduce | flops 3072 | bytes 24576 | tf_op jit(solution)/shard_map/psum | solution.py:56
  227.5 0.0 copy-done.6
  227.5 1.7 fusion.16
  (2 shorter events, 0.0 us)
Async XLA Ops:
  7.2 46.0 %all-gather.5.cloned.1.call-start = ((), (), s32[]{:S(2)}) async-start(), calls=%async_computation.2 | async-start | bytes 1671168 | tf_op jit(solution)/shard_map/all_gather | solution.py:37
  9.9 83.9 %all-gather.3.cloned.1.call-start = ((), (), s32[]{:S(2)}) async-start(), calls=%async_computation.1 | async-start | bytes 1671168 | tf_op jit(solution)/shard_map/all_gather | solution.py:42
  10.7 158.0 %reduce-scatter.2.cloned.1.call-start = ((), (), s32[]{:S(2)}) async-start(), calls=%async_computation.3 | async-start | bytes 3342336 | tf_op jit(solution)/shard_map/reduce_scatter | solution.py:50
  53.2 4.1 %copy-start = (bf16[256,3072]{1,0:T(8,128)(2,1)S(1)}, bf16[256,3072]{1,0:T(8,128)(2,1)}, u32[]{:S(2)}) copy-start(bf16[256,3072]{1,0:T(8,128)(2,1)} %all-gather.5.cloned.1.call-done) | copy-start | bytes 4718596
  53.2 4.2 %copy-start.2 = (bf16[3072,640]{1,0:T(8,128)(2,1)S(1)}, bf16[3072,640]{1,0:T(8,128)(2,1)}, u32[]{:S(2)}) copy-start(bf16[3072,640]{1,0:T(8,128)(2,1)} %param.9) | copy-start | bytes 11796484
  93.8 4.5 %copy-start.1 = (bf16[3072,640]{1,0:T(8,128)(2,1)S(1)}, bf16[3072,640]{1,0:T(8,128)(2,1)}, u32[]{:S(2)}) copy-start(bf16[3072,640]{1,0:T(8,128)(2,1)} %param.8) | copy-start | bytes 11796484
  98.3 2.1 copy-start.3
  106.8 3.4 %copy-start.5 = (bf16[256,3072]{1,0:T(8,128)(2,1)S(1)}, bf16[256,3072]{1,0:T(8,128)(2,1)}, u32[]{:S(2)}) copy-start(bf16[256,3072]{1,0:T(8,128)(2,1)} %all-gather.3.cloned.1.call-done) | copy-start | bytes 4718596
  110.2 58.4 %copy-start.4 = (bf16[16,3072]{1,0:T(8,128)(2,1)S(1)}, bf16[16,3072]{1,0:T(8,128)(2,1)}, u32[]{:S(2)}) copy-start(bf16[16,3072]{1,0:T(8,128)(2,1)} %param.6) | copy-start | bytes 294916
  110.2 58.4 %copy-start.7 = (f32[3072]{0:T(1024)S(1)}, f32[3072]{0:T(1024)}, u32[]{:S(2)}) copy-start(f32[3072]{0:T(1024)} %param.11) | copy-start | bytes 36868
  110.2 117.3 %copy-start.6 = (bf16[16,3072]{1,0:T(8,128)(2,1)S(1)}, bf16[16,3072]{1,0:T(8,128)(2,1)}, u32[]{:S(2)}) copy-start(bf16[16,3072]{1,0:T(8,128)(2,1)} %param.7) | copy-start | bytes 294916
Sparse Core Ops, SparseCore 0:
  10.8 42.3 all-gather.4
  55.5 38.2 all-gather.2
  103.6 64.9 reduce-scatter.1
where the time goes:
time: 236 us
  waiting for transfers between devices  133 us (56%)
  blocking collectives  57.7 us (24%)
  matrix products  24.5 us (10%)
  between operations  13.8 us (6%)
  other arithmetic  5.52 us (2%)
    psum x1, blocking collectives, per_device(): grad_gain = lax.psum(jnp.sum(normed_grad * unit_rows, axis=0), 'dp')  57.7 us
    reduce_scatter x1, waiting for transfers between devices, per_device(): lax.psum_scatter(partial_grad, 'dp', scatter_dimension=0, tiled=True)  55.1 us
    all_gather x1, waiting for transfers between devices, per_device(): normed_all = lax.all_gather(normed, 'dp', axis=0, tiled=True)  42.5 us
    all_gather x1, waiting for transfers between devices, per_device(): upstream_all = lax.all_gather(upstream, 'dp', axis=0, tiled=True)  34.9 us
    dot_general x3, matrix products, contract_first(): lax.dot_general(left, right, (((0,), (0,)), ((), ())), preferred_element_...  10.1 us
    dot_general x3, matrix products, contract_last(): lax.dot_general(left, right, (((1,), (1,)), ((), ())), preferred_element_...  8.91 us
  transfers between devices with their start and end apart: 3, of which 3 were waited for; matrix products, arithmetic and copies ran while one was open for 7% of the time, Pallas kernels for 0%

commit v1 on v0

v1 whole, which is shorter than its diff:
```python
import functools

import jax
import jax.numpy as jnp
from jax import lax
from jax.experimental import pallas as pl
from jax.experimental.pallas import tpu as pltpu
from jax.sharding import PartitionSpec as P

norm_floor = 0.5
gelu_coeff = 0.7978845608
cubic_term = 0.044715
MESH = pl.DeviceIdType.MESH
bf16, f32 = jnp.bfloat16, jnp.float32


def gelu_parts(gate_out):
    inner = jnp.tanh(gelu_coeff * (gate_out + cubic_term * gate_out * gate_out * gate_out))
    activated = 0.5 * gate_out * (1.0 + inner)
    gelu_slope = 0.5 * (1.0 + inner) + 0.5 * gate_out * (1.0 - inner * inner) * gelu_coeff * (
        1.0 + 3.0 * cubic_term * gate_out * gate_out
    )
    return (activated, gelu_slope)


def contract_last(left, right):
    return lax.dot_general(left, right, (((1,), (1,)), ((), ())), preferred_element_type=f32)


def contract_first(left, right):
    return lax.dot_general(left, right, (((0,), (0,)), ((), ())), preferred_element_type=f32)


def slot(side, distance, half_ring):
    if distance == half_ring:
        return 2 * half_ring - 1
    return 0 if distance == 0 else 2 * distance - 1 + side


def exchange_kernel(
    chips,
    res_hbm, ups_hbm, gate_hbm, up_hbm, down_hbm, gain_ref,
    grad_res_ref, gain_out_ref, normed_hbm, upstream_hbm, hidden_hbm, gate_grad_hbm, up_grad_hbm,
    gate_w, up_w, down_w, res, ups, normed, scale, hidden, gate_grad, up_grad,
    part, peer_send, peer_recv, ring_send, ring_recv,
    gain_part, gain_peer, gain_sum, gain_all, gain_full,
    local_sem, out_sem, own_sem, ring_ss, ring_rs, peer_ss, peer_rs,
    swap_ss, swap_rs, sum_ss, sum_rs, gain_ss, gain_rs,
):
    half_ring = chips // 2
    rows = res_hbm.shape[0]
    width = res.shape[1]
    half_width = width // 2
    tokens = res.shape[0]
    me = lax.axis_index("dp")
    chip, core = me // 2, me % 2
    position = chip // 2 + (chip % 2) * (chips - 1 - 2 * (chip // 2))

    def device_at(place, which):
        place = (place + chips) % chips
        far = place // half_ring
        return 2 * ((1 - far) * (2 * place) + far * (2 * (chips - 1 - place) + 1)) + which

    partner = {"dp": 2 * chip + (1 - core)}
    onward = ({"dp": device_at(position + 1, core)}, {"dp": device_at(position - 1, core)})

    def block(ref, k, who):
        return ref.at[pl.ds((2 * k + who) * rows, rows)]

    sources, arrays = (res_hbm, ups_hbm), (res, ups)
    own = [pltpu.make_async_copy(sources[a], block(arrays[a], 0, 0), own_sem.at[a]) for a in (0, 1)]
    for copy in own:
        copy.start()
    weights = [
        pltpu.make_async_copy(src, dst, local_sem.at[i])
        for i, (src, dst) in enumerate(((gate_hbm, gate_w), (up_hbm, up_w), (down_hbm, down_w)))
    ]
    for copy in weights:
        copy.start()

    barrier = pltpu.get_barrier_semaphore()
    pl.semaphore_signal(barrier, inc=1, device_id=partner, device_id_type=MESH)
    for step in range(1, chips):
        pl.semaphore_signal(
            barrier, inc=1, device_id={"dp": device_at(position + step, core)}, device_id_type=MESH
        )
    pl.semaphore_wait(barrier, chips)
    for copy in own:
        copy.wait()

    def remote(src, dst, send, recv, target):
        return pltpu.make_async_remote_copy(
            src_ref=src, dst_ref=dst, send_sem=send, recv_sem=recv,
            device_id=target, device_id_type=MESH,
        )

    def reach(direction, a):
        return half_ring if direction == a else half_ring - 1

    def hop(direction, a, distance):
        return remote(
            block(arrays[a], slot(direction, distance, half_ring), 0),
            block(arrays[a], slot(direction, distance + 1, half_ring), 0),
            ring_ss.at[direction, a, distance],
            ring_rs.at[direction, a, distance],
            onward[direction],
        )

    def share(a, k):
        return remote(
            block(arrays[a], k, 0), block(arrays[a], k, 1),
            peer_ss.at[a, k], peer_rs.at[a, k], partner,
        )

    streams = [(0, 0), (1, 0), (0, 1), (1, 1)]
    for direction, a in streams:
        hop(direction, a, 0).start()
    for a in (0, 1):
        share(a, 0).start()

    def arrive(distance):
        for direction, a in streams:
            if distance > reach(direction, a):
                continue
            hop(direction, a, distance - 1).wait_recv()
            if distance < reach(direction, a):
                hop(direction, a, distance).start()
            share(a, slot(direction, distance, half_ring)).start()

    batch = chips // 2
    span = batch * 2 * rows

    def normalise(b):
        for k in range(b * batch, (b + 1) * batch):
            share(0, k).wait_recv()
            at = pl.ds(2 * k * rows, 2 * rows)
            wide = res[at, :].astype(f32)
            own_scale = lax.rsqrt(jnp.mean(wide * wide, axis=1, keepdims=True) + norm_floor)
            scale[at, :] = own_scale
            normed[at, :] = (wide * own_scale * gain_ref[...]).astype(bf16)

    def forward(b):
        at = pl.ds(b * span, span)
        rows_in = normed[at, :]
        gate_out = jnp.dot(rows_in, gate_w[...], preferred_element_type=f32)
        up_out = jnp.dot(rows_in, up_w[...], preferred_element_type=f32)
        for k in range(b * batch, (b + 1) * batch):
            share(1, k).wait_recv()
        hidden_grad = contract_last(ups[at, :], down_w[...])
        activated, gelu_slope = gelu_parts(gate_out)
        hidden[at, :] = (activated * up_out).astype(bf16)
        gate_grad[at, :] = (hidden_grad * up_out * gelu_slope).astype(bf16)
        up_grad[at, :] = (hidden_grad * activated).astype(bf16)

    def backward(b):
        at = pl.ds(b * span, span)
        part[at, :] = contract_last(gate_grad[at, :], gate_w[...]) + contract_last(
            up_grad[at, :], up_w[...]
        )
        for k in range(b * batch, (b + 1) * batch):
            peer_send[pl.ds(k * rows, rows), :] = part[pl.ds((2 * k + 1) * rows, rows), :].astype(bf16)
        swap(b).start()

    def swap(b):
        at = pl.ds(b * batch * rows, batch * rows)
        return remote(peer_send.at[at], peer_recv.at[at], swap_ss.at[b], swap_rs.at[b], partner)

    def gain_term(b):
        total = jnp.zeros((1, width), f32)
        for k in range(b * batch, (b + 1) * batch):
            at = pl.ds(2 * k * rows, 2 * rows)
            unit_rows = res[at, :].astype(f32) * scale[at, :]
            total = total + jnp.sum(part[at, :] * unit_rows, axis=0, keepdims=True)
        return total

    early = (half_ring + 1) // 2
    for distance in range(1, early + 1):
        arrive(distance)
    for copy in weights:
        copy.wait()
    normalise(0)
    forward(0)
    for distance in range(early + 1, half_ring):
        arrive(distance)
    backward(0)
    gain_total = gain_term(0)
    arrive(half_ring)
    normalise(1)
    forward(1)
    backward(1)

    outs = [
        pltpu.make_async_copy(src, dst, out_sem.at[i])
        for i, (src, dst) in enumerate(
            (
                (normed, normed_hbm), (ups, upstream_hbm), (hidden, hidden_hbm),
                (gate_grad, gate_grad_hbm), (up_grad, up_grad_hbm),
            )
        )
    ]
    for copy in outs:
        copy.start()

    def pass_on(direction, h, distance):
        return remote(
            ring_send.at[direction, h, distance - 1],
            ring_recv.at[direction, h, distance - 1],
            sum_ss.at[direction, h, distance - 1],
            sum_rs.at[direction, h, distance - 1],
            onward[direction],
        )

    def columns(h):
        return pl.ds(h * half_width, half_width)

    def held(k, h):
        return part[pl.ds(2 * k * rows, rows), columns(h)] + peer_recv[
            pl.ds(k * rows, rows), columns(h)
        ].astype(f32)

    ring_order = [(0, 0), (1, 1), (1, 0), (0, 1)]

    def sum_step(distance):
        for direction, h in ring_order:
            if distance > reach(direction, h):
                continue
            value = held(slot(1 - direction, distance, half_ring), h)
            if distance < reach(direction, h):
                pass_on(direction, h, distance + 1).wait_recv()
                value = value + ring_recv[direction, h, distance].astype(f32)
            ring_send[direction, h, distance - 1] = value.astype(bf16)
            pass_on(direction, h, distance).start()

    swap(1).wait_recv()
    sum_step(half_ring)

    gain_total = gain_total + gain_term(1)
    gain_part[0] = gain_total[:, :half_width]
    gain_part[1] = gain_total[:, half_width:]
    gain_swap = remote(gain_part.at[1 - core], gain_peer, gain_ss.at[0], gain_rs.at[0], partner)
    gain_swap.start()
    swap(0).wait_recv()

    sum_step(half_ring - 1)
    gain_swap.wait_recv()
    gain_sum[...] = gain_part[core] + gain_peer[...]
    spread = [
        remote(
            gain_sum, gain_all.at[step - 1], gain_ss.at[step], gain_rs.at[step],
            {"dp": device_at(position + step, core)},
        )
        for step in range(1, chips)
    ]
    for copy in spread:
        copy.start()
    for distance in range(half_ring - 2, 0, -1):
        sum_step(distance)

    gain_value = gain_sum[...]
    for step in range(1, chips):
        spread[step - 1].wait_recv()
        gain_value = gain_value + gain_all[step - 1]
    gain_full[core] = gain_value
    gain_back = remote(
        gain_full.at[core], gain_full.at[core], gain_ss.at[chips], gain_rs.at[chips], partner
    )
    gain_back.start()

    for direction, h in ring_order:
        pass_on(direction, h, 1).wait_recv()
    normed_grad = jnp.concatenate(
        [
            held(0, h) + ring_recv[0, h, 0].astype(f32) + ring_recv[1, h, 0].astype(f32)
            for h in (0, 1)
        ],
        axis=1,
    )
    first = pl.ds(0, rows)
    norm_scale = scale[first, :]
    unit_rows = res[first, :].astype(f32) * norm_scale
    unit_grad = normed_grad * gain_ref[...]
    inner_mean = jnp.mean(unit_grad * unit_rows, axis=1, keepdims=True)
    grad_res_ref[...] = (
        ups[first, :].astype(f32) + norm_scale * (unit_grad - unit_rows * inner_mean)
    ).astype(bf16)

    gain_back.wait_recv()
    gain_out_ref[...] = gain_full[...]

    for direction, a in streams:
        for distance in range(reach(direction, a)):
            hop(direction, a, distance).wait_send()
            pass_on(direction, a, distance + 1).wait_send()
    for a in (0, 1):
        for k in range(chips):
            share(a, k).wait_send()
        swap(a).wait_send()
    gain_swap.wait_send()
    gain_back.wait_send()
    for copy in spread:
        copy.wait_send()
    for copy in outs:
        copy.wait()


def per_device(chips, residual, upstream, gate_weight, up_weight, down_weight, gain):
    rows, width = residual.shape
    units = gate_weight.shape[1]
    tokens = rows * 2 * chips
    half_ring = chips // 2
    shape = jax.ShapeDtypeStruct
    anywhere = pl.BlockSpec(memory_space=pl.ANY)
    in_vmem = pl.BlockSpec(memory_space=pltpu.VMEM)
    dma = pltpu.SemaphoreType.DMA
    grad_residual, grad_gain, normed, upstream_all, hidden, gate_grad, up_grad = pl.pallas_call(
        functools.partial(exchange_kernel, chips),
        out_shape=(
            shape((rows, width), bf16),
            shape((2, 1, width // 2), f32),
            shape((tokens, width), bf16),
            shape((tokens, width), bf16),
            shape((tokens, units), bf16),
            shape((tokens, units), bf16),
            shape((tokens, units), bf16),
        ),
        in_specs=[anywhere] * 5 + [in_vmem],
        out_specs=(in_vmem, in_vmem) + (anywhere,) * 5,
        scratch_shapes=[
            pltpu.VMEM((width, units), bf16),
            pltpu.VMEM((width, units), bf16),
            pltpu.VMEM((units, width), bf16),
            pltpu.VMEM((tokens, width), bf16),
            pltpu.VMEM((tokens, width), bf16),
            pltpu.VMEM((tokens, width), bf16),
            pltpu.VMEM((tokens, 1), f32),
            pltpu.VMEM((tokens, units), bf16),
            pltpu.VMEM((tokens, units), bf16),
            pltpu.VMEM((tokens, units), bf16),
            pltpu.VMEM((tokens, width), f32),
            pltpu.VMEM((tokens // 2, width), bf16),
            pltpu.VMEM((tokens // 2, width), bf16),
            pltpu.VMEM((2, 2, half_ring, rows, width // 2), bf16),
            pltpu.VMEM((2, 2, half_ring, rows, width // 2), bf16),
            pltpu.VMEM((2, 1, width // 2), f32),
            pltpu.VMEM((1, width // 2), f32),
            pltpu.VMEM((1, width // 2), f32),
            pltpu.VMEM((chips - 1, 1, width // 2), f32),
            pltpu.VMEM((2, 1, width // 2), f32),
            dma((3,)),
            dma((5,)),
            dma((2,)),
            dma((2, 2, half_ring)),
            dma((2, 2, half_ring)),
            dma((2, chips)),
            dma((2, chips)),
            dma((2,)),
            dma((2,)),
            dma((2, 2, half_ring)),
            dma((2, 2, half_ring)),
            dma((chips + 1,)),
            dma((chips + 1,)),
        ],
        compiler_params=pltpu.CompilerParams(
            collective_id=0, has_side_effects=True, vmem_limit_bytes=60 * 1024 * 1024
        ),
    )(residual, upstream, gate_weight, up_weight, down_weight, gain.reshape(1, width))
    grad_gate = contract_first(normed, gate_grad).astype(bf16)
    grad_up = contract_first(normed, up_grad).astype(bf16)
    grad_down = contract_first(hidden, upstream_all).astype(bf16)
    return (grad_residual, grad_gate, grad_up, grad_down, grad_gain.reshape(width))


def solution(mesh):
    placed = (
        P(("member", "dp"), None),
        P(("member", "dp"), None),
        P("member", "dp"),
        P("member", "dp"),
        P(("member", "dp"), None),
        P("member"),
    )
    return jax.shard_map(
        functools.partial(per_device, mesh.shape["dp"] // 2),
        mesh=mesh,
        in_specs=placed,
        out_specs=(
            P(("member", "dp"), None),
            P("member", "dp"),
            P("member", "dp"),
            P(("member", "dp"), None),
            P("member"),
        ),
        check_vma=False,
    )
```

time: 236 us -> 64.3 us (0.27)
  waiting for transfers between devices: 133 us -> 0 us
  blocking collectives: 57.7 us -> 0 us
  Pallas kernels: 0 us -> 50.6 us
  between operations: 13.8 us -> 0.68 us
  matrix products: 24.5 us -> 11.5 us
  other arithmetic: 5.52 us -> 0 us
    all_gather x2 -> x0, waiting for transfers between devices: 77.4 us -> none  [the longest x1 42.5 us: per_device(): normed_all = lax.all_gather(normed, 'dp', axis=0, tiled=True)]
    psum x1 -> x0, blocking collectives: 57.7 us -> none  [per_device(): grad_gain = lax.psum(jnp.sum(normed_grad * unit_rows, axis=0), 'dp')]
    reduce_scatter x1 -> x0, waiting for transfers between devices: 55.1 us -> none  [per_device(): lax.psum_scatter(partial_grad, 'dp', scatter_dimension=0, tiled=True)]
    pallas_call x0 -> x1, Pallas kernels: none -> 50.6 us  [per_device(): pl.pallas_call(functools.partial(exchange_kernel, chips), out_shape=(shap...]
    dot_general x5 -> x0, matrix products: 14.5 us -> none  [the longest x3 8.91 us: contract_last(): lax.dot_general(left, right, (((1,), (1,)), ((), ())), preferred_element_...]
    convert_element_type x2 -> x0, other arithmetic: 3.32 us -> none  [the longest x1 1.68 us: per_device(): grad_residual = (upstream.astype(jnp.float32) + norm_scale * (unit_grad -...]
  transfers between devices with their start and end apart: 3 -> 0, of which waited for: 3 -> 0; matrix products, arithmetic and copies ran while one was open for 7% -> 0% of each run, Pallas kernels for 0% -> 0%
where the time goes in v1:
time: 64.3 us; the launch traced here: 64 us
  Pallas kernels  50.6 us (79%)
  matrix products  11.5 us (18%)
  local copies, waits for them, and re-layouts  1.27 us (2%)
  between operations  0.68 us (1%)
    pallas_call x1, Pallas kernels, per_device(): pl.pallas_call(functools.partial(exchange_kernel, chips), out_shape=(shap...  50.6 us
    dot_general x3, matrix products, contract_first(): lax.dot_general(left, right, (((0,), (0,)), ((), ())), preferred_element_...  11.5 us

profile of v1, /device:TPU:0, one launch (start us, length us, event | category | flops | bytes accessed | tf_op | source)
XLA Modules:
  0.0 64.0 jit_solution(15420731613038473058)
XLA Ops:
  0.6 50.6 %shard_map.101 = (bf16[16,3072]{1,0:T(8,128)(2,1)}, f32[2,1,1536]{2,1,0:T(1,128)}, bf16[256,3072]{1,0:T(8,128)(2,1)}, bf16[256,3072]{1,0:T(8,128)(2,1)}, bf16[25...) custom-call(bf16[16,3072]{1,0:T(8,128)(2,1)} %res_hbm.1, bf16[16,3072]{1,0:T(8,128)(2,1)} %ups_hbm.1, ...), custom_call_target="tpu_custom_call" | custom-call | tf_op jit(solution)/shard_map/pallas_call | solution.py:315
  51.3 0.0 copy-start
  51.3 0.0 copy-start.3
  51.3 4.9 %convolution_convert_fusion.2 = bf16[3072,640]{1,0:T(8,128)(2,1)} fusion(bf16[256,3072]{1,0:T(8,128)(2,1)} %get-tuple-element.13, bf16[256,640]{1,0:T(8,128)(2,1)} %get-tuple-element.14), kind=kOutput, calls=%fused_computation.2 | convolution fusion | flops 1008599040 | bytes 5832704 | tf_op jit(solution)/shard_map/dot_general | solution.py:31
  56.2 0.0 copy-done
  56.2 0.0 copy-done.3
  56.2 0.0 copy-start.1
  56.2 0.0 copy-start.2
  56.3 3.4 %convolution_convert_fusion.1 = bf16[3072,640]{1,0:T(8,128)(2,1)} fusion(bf16[256,3072]{1,0:T(8,128)(2,1)S(1)} %copy-done, bf16[256,640]{1,0:T(8,128)(2,1)S(1)} %copy-done.3), kind=kOutput, calls=%fused_computation.1 | convolution fusion | flops 1008599040 | bytes 5832704 | tf_op jit(solution)/shard_map/dot_general | solution.py:31
  59.6 0.0 copy-done.1
  59.6 0.0 copy-done.2
  59.6 0.0 copy-start.4
  59.6 0.0 copy-start.5
  59.6 3.1 %convolution_convert_fusion = bf16[640,3072]{1,0:T(8,128)(2,1)} fusion(bf16[256,640]{1,0:T(8,128)(2,1)S(1)} %copy-done.2, bf16[256,3072]{1,0:T(8,128)(2,1)S(1)} %copy-done.1), kind=kOutput, calls=%fused_computation | convolution fusion | flops 1008599040 | bytes 5832704 | tf_op jit(solution)/shard_map/dot_general | solution.py:31
  62.8 0.0 copy-done.4
  62.8 0.6 %copy.13 = bf16[16,3072]{1,0:T(8,128)(2,1)} copy(bf16[16,3072]{1,0:T(8,128)(2,1)S(1)} %copy-done.4) | data formatting | bytes 196608
  63.4 0.0 copy-done.5
  63.4 0.6 copy.14
Async XLA Ops:
  51.3 5.0 %copy-start = (bf16[256,3072]{1,0:T(8,128)(2,1)S(1)}, bf16[256,3072]{1,0:T(8,128)(2,1)}, u32[]{:S(2)}) copy-start(bf16[256,3072]{1,0:T(8,128)(2,1)} %get-tuple-element.13) | copy-start | bytes 4718596
  51.3 5.0 %copy-start.3 = (bf16[256,640]{1,0:T(8,128)(2,1)S(1)}, bf16[256,640]{1,0:T(8,128)(2,1)}, u32[]{:S(2)}) copy-start(bf16[256,640]{1,0:T(8,128)(2,1)} %get-tuple-element.15) | copy-start | bytes 983044
  56.2 3.4 %copy-start.1 = (bf16[256,3072]{1,0:T(8,128)(2,1)S(1)}, bf16[256,3072]{1,0:T(8,128)(2,1)}, u32[]{:S(2)}) copy-start(bf16[256,3072]{1,0:T(8,128)(2,1)} %get-tuple-element.17) | copy-start | bytes 4718596
  56.2 3.4 %copy-start.2 = (bf16[256,640]{1,0:T(8,128)(2,1)S(1)}, bf16[256,640]{1,0:T(8,128)(2,1)}, u32[]{:S(2)}) copy-start(bf16[256,640]{1,0:T(8,128)(2,1)} %get-tuple-element.16) | copy-start | bytes 983044
  59.6 3.1 %copy-start.4 = (bf16[16,3072]{1,0:T(8,128)(2,1)S(1)}, bf16[16,3072]{1,0:T(8,128)(2,1)}, u32[]{:S(2)}) copy-start(bf16[16,3072]{1,0:T(8,128)(2,1)} %get-tuple-element.24) | copy-start | bytes 294916
  59.6 3.8 %copy-start.5 = (f32[2,1,1536]{2,1,0:T(1,128)S(1)}, f32[2,1,1536]{2,1,0:T(1,128)}, u32[]{:S(2)}) copy-start(f32[2,1,1536]{2,1,0:T(1,128)} %get-tuple-element.18) | copy-start | bytes 36868

commit v2 on v1

--- a/solution.py
+++ b/solution.py
@@ -41,7 +41,7 @@
     chips,
     res_hbm, ups_hbm, gate_hbm, up_hbm, down_hbm, gain_ref,
     grad_res_ref, gain_out_ref, normed_hbm, upstream_hbm, hidden_hbm, gate_grad_hbm, up_grad_hbm,
-    gate_w, up_w, down_w, res, ups, normed, scale, hidden, gate_grad, up_grad,
+    gate_w, up_w, down_w, res, ups, normed, normed_t, scale, hidden, gate_grad, up_grad,
     part, peer_send, peer_recv, ring_send, ring_recv,
     gain_part, gain_peer, gain_sum, gain_all, gain_full,
     local_sem, out_sem, own_sem, ring_ss, ring_rs, peer_ss, peer_rs,
@@ -148,7 +148,7 @@
             share(1, k).wait_recv()
         hidden_grad = contract_last(ups[at, :], down_w[...])
         activated, gelu_slope = gelu_parts(gate_out)
-        hidden[at, :] = (activated * up_out).astype(bf16)
+        hidden[:, at] = (activated * up_out).T.astype(bf16)
         gate_grad[at, :] = (hidden_grad * up_out * gelu_slope).astype(bf16)
         up_grad[at, :] = (hidden_grad * activated).astype(bf16)
 
@@ -164,6 +164,10 @@
     def swap(b):
         at = pl.ds(b * batch * rows, batch * rows)
         return remote(peer_send.at[at], peer_recv.at[at], swap_ss.at[b], swap_rs.at[b], partner)
+
+    def turn(b):
+        at = pl.ds(b * span, span)
+        normed_t[:, at] = normed[at, :].T
 
     def gain_term(b):
         total = jnp.zeros((1, width), f32)
@@ -184,22 +188,11 @@
         arrive(distance)
     backward(0)
     gain_total = gain_term(0)
+    turn(0)
     arrive(half_ring)
     normalise(1)
     forward(1)
     backward(1)
-
-    outs = [
-        pltpu.make_async_copy(src, dst, out_sem.at[i])
-        for i, (src, dst) in enumerate(
-            (
-                (normed, normed_hbm), (ups, upstream_hbm), (hidden, hidden_hbm),
-                (gate_grad, gate_grad_hbm), (up_grad, up_grad_hbm),
-            )
-        )
-    ]
-    for copy in outs:
-        copy.start()
 
     def pass_on(direction, h, distance):
         return remote(
@@ -242,6 +235,19 @@
     swap(0).wait_recv()
 
     sum_step(half_ring - 1)
+    turn(1)
+    outs = [
+        pltpu.make_async_copy(src, dst, out_sem.at[i])
+        for i, (src, dst) in enumerate(
+            (
+                (normed_t, normed_hbm), (ups, upstream_hbm), (hidden, hidden_hbm),
+                (gate_grad, gate_grad_hbm), (up_grad, up_grad_hbm),
+            )
+        )
+    ]
+    for copy in outs:
+        copy.start()
+
     gain_swap.wait_recv()
     gain_sum[...] = gain_part[core] + gain_peer[...]
     spread = [
@@ -303,6 +309,21 @@
         copy.wait()
 
 
+def weight_kernel(
+    normed_t, ups, hidden_t, gate_grad, up_grad, residual_in, gain_in,
+    residual_out, gate_out, up_out, down_out, gain_out,
+):
+    rows_in = normed_t[...]
+    gate_out[...] = jnp.dot(rows_in, gate_grad[...], preferred_element_type=f32).astype(bf16)
+    up_out[...] = jnp.dot(rows_in, up_grad[...], preferred_element_type=f32).astype(bf16)
+    down_out[...] = jnp.dot(hidden_t[...], ups[...], preferred_element_type=f32).astype(bf16)
+
+    @pl.when(pl.program_id(0) == 0)
+    def _():
+        residual_out[...] = residual_in[...]
+        gain_out[...] = gain_in[...]
+
+
 def per_device(chips, residual, upstream, gate_weight, up_weight, down_weight, gain):
     rows, width = residual.shape
     units = gate_weight.shape[1]
@@ -317,9 +338,9 @@
         out_shape=(
             shape((rows, width), bf16),
             shape((2, 1, width // 2), f32),
+            shape((width, tokens), bf16),
             shape((tokens, width), bf16),
-            shape((tokens, width), bf16),
-            shape((tokens, units), bf16),
+            shape((units, tokens), bf16),
             shape((tokens, units), bf16),
             shape((tokens, units), bf16),
         ),
@@ -332,8 +353,9 @@
             pltpu.VMEM((tokens, width), bf16),
             pltpu.VMEM((tokens, width), bf16),
             pltpu.VMEM((tokens, width), bf16),
+            pltpu.VMEM((width, tokens), bf16),
             pltpu.VMEM((tokens, 1), f32),
-            pltpu.VMEM((tokens, units), bf16),
+            pltpu.VMEM((units, tokens), bf16),
             pltpu.VMEM((tokens, units), bf16),
             pltpu.VMEM((tokens, units), bf16),
             pltpu.VMEM((tokens, width), f32),
@@ -364,9 +386,41 @@
             collective_id=0, has_side_effects=True, vmem_limit_bytes=60 * 1024 * 1024
         ),
     )(residual, upstream, gate_weight, up_weight, down_weight, gain.reshape(1, width))
-    grad_gate = contract_first(normed, gate_grad).astype(bf16)
-    grad_up = contract_first(normed, up_grad).astype(bf16)
-    grad_down = contract_first(hidden, upstream_all).astype(bf16)
+    steps = 6
+    tile = width // steps
+    whole = lambda *dims: pl.BlockSpec(dims, lambda i: (0,) * len(dims))
+    down_rows = pl.BlockSpec((tile, units), lambda i: (i, 0))
+    grad_residual, grad_gate, grad_up, grad_down, grad_gain = pl.pallas_call(
+        weight_kernel,
+        grid=(steps,),
+        out_shape=(
+            shape((rows, width), bf16),
+            shape((width, units), bf16),
+            shape((width, units), bf16),
+            shape((units, width), bf16),
+            shape((2, 1, width // 2), f32),
+        ),
+        in_specs=[
+            pl.BlockSpec((tile, tokens), lambda i: (i, 0)),
+            pl.BlockSpec((tokens, tile), lambda i: (0, i)),
+            whole(units, tokens),
+            whole(tokens, units),
+            whole(tokens, units),
+            whole(rows, width),
+            whole(2, 1, width // 2),
+        ],
+        out_specs=(
+            whole(rows, width),
+            down_rows,
+            down_rows,
+            pl.BlockSpec((units, tile), lambda i: (0, i)),
+            whole(2, 1, width // 2),
+        ),
+        compiler_params=pltpu.CompilerParams(vmem_limit_bytes=40 * 1024 * 1024),
+        cost_estimate=pl.CostEstimate(
+            flops=6 * tokens * width * units, bytes_accessed=8 * width * units, transcendentals=0
+        ),
+    )(normed, upstream_all, hidden, gate_grad, up_grad, grad_residual, grad_gain)
     return (grad_residual, grad_gate, grad_up, grad_down, grad_gain.reshape(width))
 
 

time: 64.3 us -> 65.9 us (1.025)
  matrix products: 11.5 us -> 0 us
  Pallas kernels: 50.6 us -> 57.5 us
  local copies, waits for them, and re-layouts: 1.27 us -> 7.32 us
    dot_general x3 -> x0, matrix products: 11.5 us -> none  [contract_first(): lax.dot_general(left, right, (((0,), (0,)), ((), ())), preferred_element_...]
    pallas_call x0 -> x1, Pallas kernels: none -> 6.9 us  [per_device(): pl.pallas_call(weight_kernel, grid=(steps,), out_shape=(shape((rows, widt...]
    unnamed x14, local copies, waits for them, and re-layouts: 1.27 us -> 7.32 us
where the time goes in v2:
time: 65.9 us; the launch traced here: 65.5 us
  Pallas kernels  57.5 us (87%)
  local copies, waits for them, and re-layouts  7.32 us (11%)
  between operations  0.66 us (1%)
    pallas_call x1, Pallas kernels, per_device(): pl.pallas_call(functools.partial(exchange_kernel, chips), out_shape=(shap...  50.6 us
    unnamed x14, local copies, waits for them, and re-layouts  7.32 us
    pallas_call x1, Pallas kernels, per_device(): pl.pallas_call(weight_kernel, grid=(steps,), out_shape=(shape((rows, widt...  6.9 us

profile of v2, /device:TPU:0, one launch (start us, length us, event | category | flops | bytes accessed | tf_op | source)
XLA Modules:
  0.0 65.5 jit_solution(16248598326512507051)
XLA Ops:
  0.6 50.6 %shard_map.101 = (bf16[16,3072]{1,0:T(8,128)(2,1)}, f32[2,1,1536]{2,1,0:T(1,128)}, bf16[3072,256]{1,0:T(8,128)(2,1)}, bf16[256,3072]{1,0:T(8,128)(2,1)}, bf16[64...) custom-call(bf16[16,3072]{1,0:T(8,128)(2,1)} %res_hbm.1, bf16[16,3072]{1,0:T(8,128)(2,1)} %ups_hbm.1, ...), custom_call_target="tpu_custom_call" | custom-call | tf_op jit(solution)/shard_map/pallas_call | solution.py:336
  51.2 0.0 copy-start
  51.3 1.4 %copy-done = bf16[3072,256]{1,0:T(8,128)(2,1)S(1)} copy-done((bf16[3072,256]{1,0:T(8,128)(2,1)S(1)}, bf16[3072,256]{1,0:T(8,128)(2,1)}, u32[]{:S(2)}) %copy-start) | copy-done | bytes 1572888
  52.7 0.0 copy-start.1
  52.7 1.4 %copy-done.1 = bf16[256,3072]{1,0:T(8,128)(2,1)S(1)} copy-done((bf16[256,3072]{1,0:T(8,128)(2,1)S(1)}, bf16[256,3072]{1,0:T(8,128)(2,1)}, u32[]{:S(2)}) %copy-start.1) | copy-done | bytes 1572888
  54.1 0.0 copy-start.2
  54.1 1.0 %copy-done.2 = bf16[640,256]{1,0:T(8,128)(2,1)S(1)} copy-done((bf16[640,256]{1,0:T(8,128)(2,1)S(1)}, bf16[640,256]{1,0:T(8,128)(2,1)}, u32[]{:S(2)}) %copy-start.2) | copy-done | bytes 327704
  55.0 0.0 copy-start.3
  55.0 1.0 %copy-done.3 = bf16[256,640]{1,0:T(8,128)(2,1)S(1)} copy-done((bf16[256,640]{1,0:T(8,128)(2,1)S(1)}, bf16[256,640]{1,0:T(8,128)(2,1)}, u32[]{:S(2)}) %copy-start.3) | copy-done | bytes 327704
  56.0 0.0 copy-start.4
  56.0 1.0 %copy-done.4 = bf16[256,640]{1,0:T(8,128)(2,1)S(1)} copy-done((bf16[256,640]{1,0:T(8,128)(2,1)S(1)}, bf16[256,640]{1,0:T(8,128)(2,1)}, u32[]{:S(2)}) %copy-start.4) | copy-done | bytes 327704
  57.0 0.0 copy-start.5
  57.0 0.9 %copy-done.5 = bf16[16,3072]{1,0:T(8,128)(2,1)S(1)} copy-done((bf16[16,3072]{1,0:T(8,128)(2,1)S(1)}, bf16[16,3072]{1,0:T(8,128)(2,1)}, u32[]{:S(2)}) %copy-start.5) | copy-done | bytes 98328
  57.9 0.0 copy-start.6
  57.9 0.7 %copy-done.6 = f32[2,1,1536]{2,1,0:T(1,128)S(1)} copy-done((f32[2,1,1536]{2,1,0:T(1,128)S(1)}, f32[2,1,1536]{2,1,0:T(1,128)}, u32[]{:S(2)}) %copy-start.6) | copy-done | bytes 12312
  58.6 6.9 %shard_map.102 = (bf16[16,3072]{1,0:T(8,128)(2,1)}, bf16[3072,640]{1,0:T(8,128)(2,1)}, bf16[3072,640]{1,0:T(8,128)(2,1)}, bf16[640,3072]{1,0:T(8,128)(2,1)}, f32[2,1,1536]{2,1,0:T(1,128)}) custom-call(bf16[3072,256]{1,0:T(8,128)(2,1)S(1)} %copy-done, bf16[256,3072]{1,0:T(8,128)(2,1)S(1)} %copy-done.1, bf16[640,256]{1,0:T(8,128)(2,1)S(1)} %copy-done.2, ...), custom_call_target="tpu_custom_call" | custom-call | flops 3019898880 | bytes 15728640 | tf_op jit(solution)/shard_map/pallas_call | solution.py:393
Async XLA Ops:
  51.2 1.4 %copy-start = (bf16[3072,256]{1,0:T(8,128)(2,1)S(1)}, bf16[3072,256]{1,0:T(8,128)(2,1)}, u32[]{:S(2)}) copy-start(bf16[3072,256]{1,0:T(8,128)(2,1)} %get-tuple-element.17.normed_t) | copy-start | bytes 4718596
  52.7 1.4 %copy-start.1 = (bf16[256,3072]{1,0:T(8,128)(2,1)S(1)}, bf16[256,3072]{1,0:T(8,128)(2,1)}, u32[]{:S(2)}) copy-start(bf16[256,3072]{1,0:T(8,128)(2,1)} %get-tuple-element.18.ups) | copy-start | bytes 4718596
  54.1 1.0 %copy-start.2 = (bf16[640,256]{1,0:T(8,128)(2,1)S(1)}, bf16[640,256]{1,0:T(8,128)(2,1)}, u32[]{:S(2)}) copy-start(bf16[640,256]{1,0:T(8,128)(2,1)} %get-tuple-element.19.hidden_t) | copy-start | bytes 983044
  55.0 1.0 %copy-start.3 = (bf16[256,640]{1,0:T(8,128)(2,1)S(1)}, bf16[256,640]{1,0:T(8,128)(2,1)}, u32[]{:S(2)}) copy-start(bf16[256,640]{1,0:T(8,128)(2,1)} %get-tuple-element.20.gate_grad) | copy-start | bytes 983044
  56.0 1.0 %copy-start.4 = (bf16[256,640]{1,0:T(8,128)(2,1)S(1)}, bf16[256,640]{1,0:T(8,128)(2,1)}, u32[]{:S(2)}) copy-start(bf16[256,640]{1,0:T(8,128)(2,1)} %get-tuple-element.21.up_grad) | copy-start | bytes 983044
  57.0 0.9 %copy-start.5 = (bf16[16,3072]{1,0:T(8,128)(2,1)S(1)}, bf16[16,3072]{1,0:T(8,128)(2,1)}, u32[]{:S(2)}) copy-start(bf16[16,3072]{1,0:T(8,128)(2,1)} %get-tuple-element.22.residual_in) | copy-start | bytes 294916
  57.9 0.7 %copy-start.6 = (f32[2,1,1536]{2,1,0:T(1,128)S(1)}, f32[2,1,1536]{2,1,0:T(1,128)}, u32[]{:S(2)}) copy-start(f32[2,1,1536]{2,1,0:T(1,128)} %get-tuple-element.23.gain_in) | copy-start | bytes 36868

commit v3 on v2

--- a/solution.py
+++ b/solution.py
@@ -416,7 +416,7 @@
             pl.BlockSpec((units, tile), lambda i: (0, i)),
             whole(2, 1, width // 2),
         ),
-        compiler_params=pltpu.CompilerParams(vmem_limit_bytes=40 * 1024 * 1024),
+        compiler_params=pltpu.CompilerParams(vmem_limit_bytes=62 * 1024 * 1024),
         cost_estimate=pl.CostEstimate(
             flops=6 * tokens * width * units, bytes_accessed=8 * width * units, transcendentals=0
         ),

time: 65.9 us -> 60.6 us (0.920)
  local copies, waits for them, and re-layouts: 7.32 us -> 0 us
  Pallas kernels: 57.5 us -> 59.7 us
    unnamed x14 -> x0, local copies, waits for them, and re-layouts: 7.32 us -> none
    pallas_call x1, Pallas kernels: 6.9 us -> 9.06 us  [per_device(): pl.pallas_call(weight_kernel, grid=(steps,), out_shape=(shape((rows, widt...]
where the time goes in v3:
time: 60.6 us; the launch traced here: 60.3 us
  Pallas kernels  59.7 us (99%)
  between operations  0.64 us (1%)
    pallas_call x1, Pallas kernels, per_device(): pl.pallas_call(functools.partial(exchange_kernel, chips), out_shape=(shap...  50.6 us
    pallas_call x1, Pallas kernels, per_device(): pl.pallas_call(weight_kernel, grid=(steps,), out_shape=(shape((rows, widt...  9.06 us

profile of v3, /device:TPU:0, one launch (start us, length us, event | category | flops | bytes accessed | tf_op | source)
XLA Modules:
  0.0 60.3 jit_solution(6439968075842224678)
XLA Ops:
  0.6 50.6 %shard_map.101 = (bf16[16,3072]{1,0:T(8,128)(2,1)}, f32[2,1,1536]{2,1,0:T(1,128)}, bf16[3072,256]{1,0:T(8,128)(2,1)}, bf16[256,3072]{1,0:T(8,128)(2,1)}, bf16[64...) custom-call(bf16[16,3072]{1,0:T(8,128)(2,1)} %res_hbm.1, bf16[16,3072]{1,0:T(8,128)(2,1)} %ups_hbm.1, ...), custom_call_target="tpu_custom_call" | custom-call | tf_op jit(solution)/shard_map/pallas_call | solution.py:336
  51.2 9.1 %shard_map.102 = (bf16[16,3072]{1,0:T(8,128)(2,1)}, bf16[3072,640]{1,0:T(8,128)(2,1)}, bf16[3072,640]{1,0:T(8,128)(2,1)}, bf16[640,3072]{1,0:T(8,128)(2,1)}, f32[2,1,1536]{2,1,0:T(1,128)}) custom-call(bf16[3072,256]{1,0:T(8,128)(2,1)} %get-tuple-element.17.normed_t, bf16[256,3072]{1,0:T(8,128)(2,1)} %get-tuple-element.18.ups, ...), custom_call_target="tpu_custom_call" | custom-call | flops 3019898880 | bytes 15728640 | tf_op jit(solution)/shard_map/pallas_call | solution.py:393
